TPU v7x, 32 devices: a whole 2x2x4 slice. The times are simulated.
32 devices in a mesh: sub: 16 (over z, y, x), crs: 2 (over core).
Axes of the slice: x: 2, y: 2, z: 4, core: 2. Of those that a mesh axis runs over, the one named last changes fastest.
Arguments:
- multipliers: float32 [16, 128, 512], P(None, ('sub', 'crs')), may hold values from -6 to 6
- own_modes: float32 [6, 128, 512], P(None, ('sub', 'crs')), may hold values from -0.75 to 0.75
- neighbour_modes: float32 [6, 128, 512], P(None, ('sub', 'crs')), may hold values from -0.75 to 0.75
- face_index: int32 [128, 512], P(('sub', 'crs')), may hold values from 0 to 5, as said below
- neighbour_list: int32 [128, 6], replicated, may hold values from 0 to 127, as said below
- coarse_factor: float32 [768, 768], P('sub', 'crs'), may hold values from -0.21875 to 0.21875
Outputs:
- projected: float32 [16, 128, 512], P(None, ('sub', 'crs'))
Inputs may be any that keep to these rules, and one draw needn't show every extreme that they name: `face_index`: the multipliers of each subdomain lie in 6 contiguous nonempty blocks, face 0 first and face 5 last. `neighbour_list`: subdomain s = (8 x + y) * 8 + z sits at (x, y, z) of a periodic grid of 2 x 8 x 8 subdomains; the 6 faces of each subdomain name its grid neighbours x plus 1, x minus 1, y plus or minus 1, z plus or minus 1 (periodic; along the first dimension both name the same subdomain), in an order that differs from subdomain to subdomain.
All inputs are finite; a program needn't handle non-finite values.
Results may differ from a plain program's by a relative error of at most 0.0001.
Values sent between devices are 32-bit elements; how exact they have to be, the bound alone decides.
A program may use at most 64 MiB of HBM per device.

v0:
```python
import functools

import jax
import jax.numpy as jnp
from jax import lax
from jax.experimental import pallas as pl
from jax.experimental.pallas import tpu as pltpu
from jax.sharding import PartitionSpec as P

MESH = pl.DeviceIdType.MESH
NT = (((1,), (1,)), ((), ()))
NN = (((1,), (0,)), ((), ()))
LANES = 128
EDGE = 8


def each(count, step):
    if count <= 64:
        for i in sorted(range(count), key=lambda i: min(i, count - 1 - i)):
            step(i)
    else:
        lax.fori_loop(0, count, lambda i, t: (step(i), t)[1], 0)


def both(value, axis=0):
    high = value.astype(jnp.bfloat16)
    low = (value - high.astype(jnp.float32)).astype(jnp.bfloat16)
    return jnp.concatenate([high, low], axis=axis)


def halves(value):
    rows = value.shape[0] // 2
    return value[:rows] + value[rows:]


def quarters(value):
    value = halves(value)
    cols = value.shape[1] // 2
    return value[:, :cols] + value[:, cols:]


def dot(left, right, dims):
    return lax.dot_general(left, right, dims, preferred_element_type=jnp.float32)


def twice(left, right):
    high = left.astype(jnp.bfloat16)
    low = (left - high.astype(jnp.float32)).astype(jnp.bfloat16)
    wide = jnp.concatenate(
        [jnp.concatenate([high, high], axis=1), jnp.concatenate([low, low], axis=1)], axis=0)
    return halves(dot(wide, right, NN))


def kernel(
    sub_size, crs_size,
    mult_h, own_h, nbr_h, face_h, nlist_h, factor_h, out_h,
    mult, own, nbr, face, nlist, factor,
    modes, pair, c_send, c_recv, fcat, fown, fpair, rs_send, rs_recv, ag_send, panel,
    c_ssem, c_rsem, f_ssem, f_rsem, rs_ssem, rs_rsem, ag_ssem, ag_rsem, in_sem, met,
):
    nk, subs, width = own.shape
    nrhs = mult.shape[0]
    nface = nlist.shape[0]
    part = nk * subs
    parts = sub_size // nrhs
    row_len = sub_size // 2
    group = subs * crs_size
    devices = sub_size * crs_size
    g = lax.axis_index("sub")
    c = lax.axis_index("crs")
    me = g * crs_size + c
    up, down = part, part + EDGE
    off_x = part + 2 * EDGE
    off_n, off_p = off_x + part, off_x + 2 * part

    def rank(i):
        other = lax.rem(me + i, devices)
        return (other // crs_size, lax.rem(other, crs_size))

    loads = [
        pltpu.make_async_copy(a, b, in_sem.at[i]) for i, (a, b) in enumerate((
            (nlist_h, nlist), (face_h, face), (nbr_h, nbr), (own_h, own),
            (mult_h, mult), (factor_h, factor)))
    ]
    for load in loads:
        load.start()
    barrier = pltpu.get_barrier_semaphore()
    first, second = g // row_len, lax.rem(g, row_len)
    across = lax.rem(first + 1, 2) * row_len + second
    after = first * row_len + lax.rem(second + 1, row_len)
    before = first * row_len + lax.rem(second + row_len - 1, row_len)
    groups = (g, across, after, before)

    block = 1 << (devices.bit_length() // 2)
    base = me // block * block
    inner = [base + lax.rem(me - base + i, block) for i in range(1, block)]
    outer = [lax.rem(me + i, devices) for i in range(block, devices, block)]
    near = [groups[j] * crs_size + lax.rem(c + i, crs_size)
            for j in range(4) for i in range(crs_size) if j or i]

    def signal(semaphore, other):
        pl.semaphore_signal(
            semaphore, inc=1, device_id=(other // crs_size, lax.rem(other, crs_size)),
            device_id_type=MESH)

    for other in outer + near + inner:
        signal(barrier, other)

    modes[...] = jnp.zeros_like(modes)
    fcat[:, down + EDGE + 3 * part:, :] = jnp.zeros(
        (crs_size, LANES - (down + EDGE + 3 * part), fcat.shape[2]), jnp.float32)
    for load in loads[:4]:
        load.wait()
    fc = face[...]
    first_sub = me * subs
    line = lax.broadcasted_iota(jnp.int32, (subs, width), 0)
    target = jnp.zeros((subs, width), jnp.int32)
    for f in range(nface):
        name = jnp.zeros((subs, width), jnp.int32)
        for s in range(subs):
            name = jnp.where(line == s, nlist[f, first_sub + s], name)
        target = jnp.where(fc == f, name, target)
    third = c * subs + line
    nxt = jnp.where(third == group - 1, 0, third + 1)
    prv = jnp.where(third == 0, group - 1, third - 1)

    def chosen(block, line):
        return jnp.where(target == block * group + line, 1.0, 0.0)

    masks = (
        chosen(g, nxt), chosen(g, prv),
        chosen(across, third), chosen(after, third), chosen(before, third),
    )
    for s in range(subs):
        cols = pl.ds(s * width, width)
        own_s = own[:, s, :]
        nbr_s = nbr[:, s, :]
        rows = (
            nk * (s + 1) if s < subs - 1 else up,
            nk * (s - 1) if s > 0 else down + EDGE - nk,
            off_x + nk * s, off_n + nk * s, off_p + nk * s,
        )
        modes[pl.ds(nk * s, nk), cols] = own_s
        for d in range(5):
            value = nbr_s * masks[d][s:s + 1, :]
            spot = pl.ds(rows[d], nk)
            modes[spot, cols] = value
    loads[4].wait()
    sums = jnp.zeros((2 * nrhs, 2 * LANES), jnp.float32)
    for s in range(subs):
        cols = pl.ds(s * width, width)
        split = both(modes[:, cols])
        pair[:, cols] = split
        sums = sums + dot(both(mult[:, s, :]), split, NT)
    sums = quarters(sums)
    c_send[...] = sums
    c_recv[0, c] = sums

    pl.semaphore_wait(barrier, len(outer) + len(near) + len(inner))

    def c_copy(j, i):
        to = lax.rem(c + i, crs_size)
        return pltpu.make_async_remote_copy(
            src_ref=c_send, dst_ref=c_recv.at[j, c],
            send_sem=c_ssem.at[j, i], recv_sem=c_rsem.at[j, i],
            device_id=(groups[j], to), device_id_type=MESH)

    def c_wait(j, i):
        src = lax.rem(c + crs_size - i, crs_size)
        pltpu.make_async_remote_copy(
            src_ref=c_send, dst_ref=c_recv.at[j, src],
            send_sem=c_ssem.at[j, i], recv_sem=c_rsem.at[j, i],
            device_id=(groups[j], src), device_id_type=MESH).wait_recv()

    for j in (1, 2, 3, 0):
        for i in range(crs_size):
            if j or i:
                c_copy(j, i).start()

    def row(p, extra=0):
        return pl.multiple_of(p * part + extra, 8)

    def f_pieces(i):
        to = lax.rem(c + i, crs_size)
        nx = lax.rem(to + 1, crs_size)
        pv = lax.rem(to + crs_size - 1, crs_size)
        return to, (
            (row(to), 0, part, g),
            (row(nx), up, EDGE, g),
            (row(pv, part - EDGE), down, EDGE, g),
            (row(to), off_x, part, across),
            (row(to), off_p, part, after),
            (row(to), off_n, part, before),
        )

    def f_copy(i, n):
        to, pieces = f_pieces(i)
        start, place, size, where = pieces[n]
        return pltpu.make_async_remote_copy(
            src_ref=factor.at[pl.ds(start, size), :],
            dst_ref=fcat.at[c, pl.ds(place, size), :],
            send_sem=f_ssem.at[i, n], recv_sem=f_rsem.at[i, n],
            device_id=(where, to), device_id_type=MESH)

    def f_wait(i, n):
        to, pieces = f_pieces(i)
        start, place, size, where = pieces[n]
        src = lax.rem(c + crs_size - i, crs_size)
        pltpu.make_async_remote_copy(
            src_ref=factor.at[pl.ds(start, size), :],
            dst_ref=fcat.at[src, pl.ds(place, size), :],
            send_sem=f_ssem.at[i, n], recv_sem=f_rsem.at[i, n],
            device_id=(where, to), device_id_type=MESH).wait_recv()

    for other in outer:
        signal(met, other)

    loads[5].wait()
    span = LANES // part
    blocks = fown.shape[0]
    for b in range(blocks):
        held = factor[b * span * part:min((b + 1) * span, crs_size) * part, :]
        if held.shape[0] < LANES:
            held = jnp.concatenate(
                [held, jnp.zeros((LANES - held.shape[0], held.shape[1]), jnp.float32)], axis=0)
        fown[b] = both(held)

    for j in (0, 1, 2, 3):
        for i in range(crs_size):
            if j or i:
                c_wait(j, i)

    lane = lax.broadcasted_iota(jnp.int32, (nrhs, LANES), 1)

    def rolled(value, by):
        return pltpu.roll(value, (LANES - by) % LANES, 1) if by % LANES else value

    total = jnp.zeros((nrhs, factor.shape[1]), jnp.float32)
    for b in range(blocks):
        group_rhs = jnp.zeros((nrhs, LANES), jnp.float32)
        for p in range(b * span, min((b + 1) * span, crs_size)):
            at = (p - b * span) * part
            low = c_recv[0, (p - 1) % crs_size]
            high = c_recv[0, (p + 1) % crs_size]
            rhs = rolled(c_recv[0, p], -at)
            rhs = rhs + jnp.where(lane < at + EDGE, rolled(low, up - at), 0.0)
            rhs = rhs + jnp.where(
                lane >= at + part - EDGE, rolled(high, down - (at + part - EDGE)), 0.0)
            rhs = rhs + rolled(c_recv[1, p], off_x - at)
            rhs = rhs + rolled(c_recv[2, p], off_n - at)
            rhs = rhs + rolled(c_recv[3, p], off_p - at)
            group_rhs = jnp.where((lane >= at) & (lane < at + part), rhs, group_rhs)
        total = total + twice(group_rhs, fown[b])

    chunk = factor.shape[1] // parts
    for q in range(parts):
        for r in range(nrhs):
            rs_send[q * nrhs + r] = total[r:r + 1, q * chunk:(q + 1) * chunk]

    def rs_copy(i):
        to = lax.rem(g + i, sub_size)
        return pltpu.make_async_remote_copy(
            src_ref=rs_send.at[to], dst_ref=rs_recv.at[g],
            send_sem=rs_ssem.at[i], recv_sem=rs_rsem.at[i],
            device_id=(to, c), device_id_type=MESH)

    def rs_wait(i):
        src = lax.rem(g + sub_size - i, sub_size)
        pltpu.make_async_remote_copy(
            src_ref=rs_send.at[src], dst_ref=rs_recv.at[src],
            send_sem=rs_ssem.at[i], recv_sem=rs_rsem.at[i],
            device_id=(src, c), device_id_type=MESH).wait_recv()

    pl.semaphore_wait(met, len(outer))
    each(sub_size - 1, lambda i: rs_copy(i + 1).start())
    moves = [(i, n) for i in range(crs_size) for n in range(6) if i or n > 2]
    for i, n in moves:
        f_copy(i, n).start()
    _, pieces = f_pieces(0)
    for start, place, size, _ in pieces[:3]:
        fcat[c, pl.ds(place, size), :] = factor[pl.ds(start, size), :]

    rs_recv[g] = rs_send[g]
    each(sub_size - 1, lambda i: rs_wait(i + 1))
    mine = rs_recv[0]
    for q in range(1, sub_size):
        mine = mine + rs_recv[q]
    ag_send[...] = mine

    def ag_copy(i):
        return pltpu.make_async_remote_copy(
            src_ref=ag_send, dst_ref=panel.at[c, g],
            send_sem=ag_ssem.at[i], recv_sem=ag_rsem.at[i],
            device_id=rank(i), device_id_type=MESH)

    def ag_wait(i):
        fg, fcr = rank(devices - i)
        pltpu.make_async_remote_copy(
            src_ref=ag_send, dst_ref=panel.at[fcr, fg],
            send_sem=ag_ssem.at[i], recv_sem=ag_rsem.at[i],
            device_id=(fg, fcr), device_id_type=MESH).wait_recv()

    each(devices - 1, lambda i: ag_copy(i + 1).start())
    panel[c, g] = mine
    for i, n in moves:
        f_wait(i, n)
    for p in range(crs_size):
        fpair[p] = both(fcat[p])
    each(devices - 1, lambda i: ag_wait(i + 1))

    amps = jnp.zeros((2 * nrhs, 2 * LANES), jnp.float32)
    for p in range(crs_size):
        for q in range(parts):
            rows = panel[p, q * nrhs:(q + 1) * nrhs].reshape(nrhs, chunk)
            amps = amps + dot(both(rows), fpair[p, :, q * chunk:(q + 1) * chunk], NT)
    amps = quarters(amps)
    for s in range(subs):
        out_h[:, s, :] = twice(amps, pair[:, s * width:(s + 1) * width])

    for j in range(4):
        for i in range(crs_size):
            if j or i:
                c_copy(j, i).wait_send()
    for i, n in moves:
        f_copy(i, n).wait_send()
    each(sub_size - 1, lambda i: rs_copy(i + 1).wait_send())
    each(devices - 1, lambda i: ag_copy(i + 1).wait_send())


def body(sub_size, crs_size, mult, own, nbr, face, nlist, factor):
    nk, subs, width = own.shape
    nrhs = mult.shape[0]
    part = nk * subs
    blocks = -(-crs_size // (LANES // part))
    cols = factor.shape[1]
    chunk = cols * nrhs // sub_size
    f32 = jnp.float32
    dma = pltpu.SemaphoreType.DMA
    bf16 = jnp.bfloat16
    hbm = pl.BlockSpec(memory_space=pl.ANY)
    names = nlist.T
    applied = pl.pallas_call(
        functools.partial(kernel, sub_size, crs_size),
        out_shape=pltpu.VMEM(mult.shape, mult.dtype),
        in_specs=[hbm] * 6,
        out_specs=pl.BlockSpec(memory_space=pltpu.VMEM),
        scratch_shapes=[
            pltpu.VMEM(mult.shape, f32), pltpu.VMEM(own.shape, f32), pltpu.VMEM(nbr.shape, f32),
            pltpu.VMEM(face.shape, face.dtype), pltpu.SMEM(names.shape, names.dtype),
            pltpu.VMEM(factor.shape, f32),
            pltpu.VMEM((LANES, subs * width), f32),
            pltpu.VMEM((2 * LANES, subs * width), bf16),
            pltpu.VMEM((nrhs, LANES), f32),
            pltpu.VMEM((4, crs_size, nrhs, LANES), f32),
            pltpu.VMEM((crs_size, LANES, cols), f32),
            pltpu.VMEM((blocks, 2 * LANES, cols), bf16),
            pltpu.VMEM((crs_size, 2 * LANES, cols), bf16),
            pltpu.VMEM((sub_size, 1, chunk), f32),
            pltpu.VMEM((sub_size, 1, chunk), f32),
            pltpu.VMEM((1, chunk), f32),
            pltpu.VMEM((crs_size, sub_size, 1, chunk), f32),
            dma((4, crs_size)), dma((4, crs_size)),
            dma((crs_size, 6)), dma((crs_size, 6)),
            dma((sub_size,)), dma((sub_size,)),
            dma((sub_size * crs_size,)), dma((sub_size * crs_size,)), dma((6,)),
            pltpu.SemaphoreType.REGULAR,
        ],
        compiler_params=pltpu.CompilerParams(collective_id=0, has_side_effects=True),
    )(mult, own, nbr, face, names, factor)
    return mult - applied


def solution(mesh):
    placed = (
        P(None, ("sub", "crs"), None),
        P(None, ("sub", "crs"), None),
        P(None, ("sub", "crs"), None),
        P(("sub", "crs"), None),
        P(),
        P("sub", "crs"),
    )
    return jax.shard_map(
        functools.partial(body, mesh.shape["sub"], mesh.shape["crs"]),
        mesh=mesh, in_specs=placed, out_specs=P(None, ("sub", "crs"), None), check_vma=False
    )
```

profile of v0, /device:TPU:0, one launch (start us, length us, event | category | flops | bytes accessed | tf_op | source)
XLA Modules:
  0.0 21.5 jit_solution(17405810119997864591)
XLA Ops:
  0.0 0.0 copy-start
  0.0 20.8 %shard_map.64 = f32[16,4,512]{2,1,0:T(4,128)S(1)} custom-call(f32[16,4,512]{2,1,0:T(4,128)} %mult_h.1, f32[6,4,512]{2,1,0:T(4,128)} %own_h.1, f32[6,4,512]{2,1,0:T(4,128)} %nbr_h.1, s32[4,512]{1,0:T(4,128)} %face_h.1, s32[6,128]{1,0:T(8,128)} %bitcast.1, f32[48,384]{1,0:T(8,128)} %factor_h.1), custom_call_target="tpu_custom_call" | custom-call | tf_op jit(solution)/shard_map/pallas_call | solution.py:342
  20.8 0.0 copy-done
  20.8 0.7 %sub.3 = f32[16,4,512]{2,1,0:T(4,128)} subtract(f32[16,4,512]{2,1,0:T(4,128)S(1)} %copy-done, f32[16,4,512]{2,1,0:T(4,128)S(1)} %shard_map.64) | non-fusion elementwise | flops 32768 | bytes 393216 | tf_op jit(solution)/shard_map/sub | solution.py:370
Async XLA Ops:
  0.0 20.8 %copy-start = (f32[16,4,512]{2,1,0:T(4,128)S(1)}, f32[16,4,512]{2,1,0:T(4,128)}, u32[]{:S(2)}) copy-start(f32[16,4,512]{2,1,0:T(4,128)} %mult_h.1) | copy-start | bytes 393220
where the time goes:
time: 21.6 us; the launch traced here: 21.5 us
  Pallas kernels  20.8 us (96%)
  other arithmetic  0.69 us (3%)
    pallas_call x1, Pallas kernels, body(): pl.pallas_call(functools.partial(kernel, sub_size, crs_size), out_shape=p...  20.8 us
    sub x1, other arithmetic, body(): return mult - applied  0.69 us

commit v1 on v0

--- a/solution.py
+++ b/solution.py
@@ -51,7 +51,321 @@
     return halves(dot(wide, right, NN))
 
 
-def kernel(
+def near_kernel(
+    sub_size, crs_size,
+    mult_h, own_h, nbr_h, face_h, nlist_h, factor_h, out_h,
+    mult, own, nbr, face, nlist, factor,
+    modes, pair, c_send, c_recv, fcat, fall, fown, fpair, p_send, p_recv, s_send, panel,
+    in_sem, c_ssem, c_rsem, g_ssem, g_rsem, f_ssem, f_rsem, p_ssem, p_rsem, s_ssem, s_rsem,
+):
+    nk, subs, width = own.shape
+    nrhs = mult.shape[0]
+    nface = nlist.shape[0]
+    part = nk * subs
+    cols = factor.shape[1]
+    tiles = cols // LANES
+    slabs = crs_size * tiles
+    row_len = sub_size // 2
+    group = subs * crs_size
+    devices = sub_size * crs_size
+    head = crs_size - 1
+    g = lax.axis_index("sub")
+    c = lax.axis_index("crs")
+    me = g * crs_size + c
+    is_head = c == head
+    is_owner = jnp.logical_and(is_head, g < slabs)
+    up, down = part, part + EDGE
+    off_x = part + 2 * EDGE
+    off_n, off_p = off_x + part, off_x + 2 * part
+
+    loads = [
+        pltpu.make_async_copy(a, b, in_sem.at[i]) for i, (a, b) in enumerate((
+            (nlist_h, nlist), (face_h, face), (nbr_h, nbr), (own_h, own),
+            (mult_h, mult), (factor_h, factor)))
+    ]
+    for load in loads:
+        load.start()
+    barrier = pltpu.get_barrier_semaphore()
+    first, second = g // row_len, lax.rem(g, row_len)
+    across = lax.rem(first + 1, 2) * row_len + second
+    after = first * row_len + lax.rem(second + 1, row_len)
+    before = first * row_len + lax.rem(second + row_len - 1, row_len)
+    groups = (g, across, after, before)
+    near = [(groups[j], lax.rem(c + i, crs_size))
+            for j in range(4) for i in range(crs_size) if j or i]
+
+    def signal(to):
+        pl.semaphore_signal(barrier, inc=1, device_id=to, device_id_type=MESH)
+
+    for to in near:
+        signal(to)
+
+    @pl.when(is_owner)
+    def _():
+        for i in range(1, sub_size):
+            signal((lax.rem(g + i, sub_size), head))
+
+    modes[...] = jnp.zeros_like(modes)
+    edge = down + EDGE + 3 * part
+    for p in range(crs_size):
+        fcat[pl.ds(p * LANES + edge, LANES - edge), :] = jnp.zeros((LANES - edge, cols), jnp.float32)
+    for load in loads[:4]:
+        load.wait()
+    fc = face[...]
+    first_sub = me * subs
+    line = lax.broadcasted_iota(jnp.int32, (subs, width), 0)
+    target = jnp.zeros((subs, width), jnp.int32)
+    for f in range(nface):
+        name = jnp.zeros((subs, width), jnp.int32)
+        for s in range(subs):
+            name = jnp.where(line == s, nlist[f, first_sub + s], name)
+        target = jnp.where(fc == f, name, target)
+    third = c * subs + line
+    nxt = jnp.where(third == group - 1, 0, third + 1)
+    prv = jnp.where(third == 0, group - 1, third - 1)
+
+    def chosen(block, line):
+        return jnp.where(target == block * group + line, 1.0, 0.0)
+
+    masks = (
+        chosen(g, nxt), chosen(g, prv),
+        chosen(across, third), chosen(after, third), chosen(before, third),
+    )
+    for s in range(subs):
+        at = pl.ds(s * width, width)
+        own_s = own[:, s, :]
+        nbr_s = nbr[:, s, :]
+        rows = (
+            nk * (s + 1) if s < subs - 1 else up,
+            nk * (s - 1) if s > 0 else down + EDGE - nk,
+            off_x + nk * s, off_n + nk * s, off_p + nk * s,
+        )
+        modes[pl.ds(nk * s, nk), at] = own_s
+        for d in range(5):
+            modes[pl.ds(rows[d], nk), at] = nbr_s * masks[d][s:s + 1, :]
+    loads[4].wait()
+    sums = jnp.zeros((2 * nrhs, 2 * LANES), jnp.float32)
+    for s in range(subs):
+        at = pl.ds(s * width, width)
+        split = both(modes[:, at])
+        pair[:, at] = split
+        sums = sums + dot(both(mult[:, s, :]), split, NT)
+    sums = quarters(sums)
+    c_send[...] = sums
+
+    @pl.when(is_head)
+    def _():
+        c_recv[c] = sums
+
+    loads[5].wait()
+
+    @pl.when(is_owner)
+    def _():
+        pl.semaphore_wait(barrier, len(near) + slabs - 1)
+
+    @pl.when(jnp.logical_and(is_head, g >= slabs))
+    def _():
+        pl.semaphore_wait(barrier, len(near) + slabs)
+
+    @pl.when(jnp.logical_not(is_head))
+    def _():
+        pl.semaphore_wait(barrier, len(near))
+
+    def c_copy(j):
+        return pltpu.make_async_remote_copy(
+            src_ref=c_send, dst_ref=c_recv.at[j * crs_size + c],
+            send_sem=c_ssem, recv_sem=c_rsem,
+            device_id=(groups[j], head), device_id_type=MESH)
+
+    def landed(ref, semaphore):
+        pltpu.make_async_copy(ref, ref, semaphore).wait()
+
+    for j in (1, 2, 3):
+        c_copy(j).start()
+
+    def g_copy():
+        return pltpu.make_async_remote_copy(
+            src_ref=factor, dst_ref=fall.at[c],
+            send_sem=g_ssem, recv_sem=g_rsem,
+            device_id=(g, head), device_id_type=MESH)
+
+    @pl.when(jnp.logical_not(is_head))
+    def _():
+        c_copy(0).start()
+        g_copy().start()
+
+    def row(p, extra=0):
+        return pl.multiple_of(p * part + extra, 8)
+
+    def f_pieces(i):
+        to = lax.rem(c + i, crs_size)
+        nx = lax.rem(to + 1, crs_size)
+        pv = lax.rem(to + crs_size - 1, crs_size)
+        return to, (
+            (row(to), 0, part, g),
+            (row(nx), up, EDGE, g),
+            (row(pv, part - EDGE), down, EDGE, g),
+            (row(to), off_x, part, across),
+            (row(to), off_p, part, after),
+            (row(to), off_n, part, before),
+        )
+
+    def place(ref, p, start, size):
+        return ref.at[pl.ds(pl.multiple_of(p * LANES + start, 8), size), :]
+
+    moved = 0
+    for i in range(crs_size):
+        to, pieces = f_pieces(i)
+        for n, (start, spot, size, where) in enumerate(pieces):
+            if i or n > 2:
+                moved += size
+                pltpu.make_async_remote_copy(
+                    src_ref=factor.at[pl.ds(start, size), :],
+                    dst_ref=place(fcat, c, spot, size),
+                    send_sem=f_ssem, recv_sem=f_rsem,
+                    device_id=(where, to), device_id_type=MESH).start()
+    _, pieces = f_pieces(0)
+    for start, spot, size, _ in pieces[:3]:
+        fcat[pl.ds(pl.multiple_of(c * LANES + spot, 8), size), :] = factor[pl.ds(start, size), :]
+
+    lane = lax.broadcasted_iota(jnp.int32, (nrhs, LANES), 1)
+
+    def rolled(value, by):
+        return pltpu.roll(value, (LANES - by) % LANES, 1) if by % LANES else value
+
+    def p_copy(j):
+        return pltpu.make_async_remote_copy(
+            src_ref=p_send.at[j], dst_ref=p_recv.at[g],
+            send_sem=p_ssem, recv_sem=p_rsem,
+            device_id=(j, head), device_id_type=MESH)
+
+    @pl.when(is_head)
+    def _():
+        held = part * crs_size
+        spare = jnp.zeros((LANES - held, cols), jnp.float32)
+        fown[head] = both(jnp.concatenate([factor[...], spare], axis=0))
+        landed(fall.at[pl.ds(0, head)], g_rsem)
+        for p in range(head):
+            fown[p] = both(jnp.concatenate([fall[p], spare], axis=0))
+        landed(c_recv.at[pl.ds(0, 4 * crs_size - 1)], c_rsem)
+        rhs = jnp.zeros((nrhs, LANES), jnp.float32)
+        for p in range(crs_size):
+            at = p * part
+            low = c_recv[(p - 1) % crs_size]
+            high = c_recv[(p + 1) % crs_size]
+            mine = rolled(c_recv[p], -at)
+            mine = mine + jnp.where(lane < at + EDGE, rolled(low, up - at), 0.0)
+            mine = mine + jnp.where(
+                lane >= at + part - EDGE, rolled(high, down - (at + part - EDGE)), 0.0)
+            mine = mine + rolled(c_recv[crs_size + p], off_x - at)
+            mine = mine + rolled(c_recv[2 * crs_size + p], off_n - at)
+            mine = mine + rolled(c_recv[3 * crs_size + p], off_p - at)
+            rhs = jnp.where((lane >= at) & (lane < at + part), mine, rhs)
+        for p in range(crs_size):
+            term = twice(rhs, fown[p])
+            for t in range(tiles):
+                p_send[p * tiles + t] = term[:, t * LANES:(t + 1) * LANES]
+        for j in range(slabs):
+            @pl.when(g != j)
+            def _():
+                p_copy(j).start()
+
+    landed(fcat.at[pl.ds(0, moved), :], f_rsem)
+    for p in range(crs_size):
+        fpair[p] = both(fcat[pl.ds(p * LANES, LANES), :])
+
+    def s_copy(t):
+        to = t + jnp.where(t >= me, 1, 0)
+        return pltpu.make_async_remote_copy(
+            src_ref=s_send, dst_ref=panel.at[g],
+            send_sem=s_ssem, recv_sem=s_rsem,
+            device_id=(to // crs_size, lax.rem(to, crs_size)), device_id_type=MESH)
+
+    @pl.when(is_owner)
+    def _():
+        p_recv[g] = p_send[g]
+        landed(p_recv.at[pl.ds(0, sub_size - 1)], p_rsem)
+        mine = p_recv[0]
+        for q in range(1, sub_size):
+            mine = mine + p_recv[q]
+        s_send[...] = mine
+        panel[g] = mine
+        for t in range(devices - 1):
+            s_copy(t).start()
+        landed(panel.at[pl.ds(0, slabs - 1)], s_rsem)
+
+    @pl.when(jnp.logical_not(is_owner))
+    def _():
+        landed(panel, s_rsem)
+
+    amps = jnp.zeros((2 * nrhs, 2 * LANES), jnp.float32)
+    for j in range(slabs):
+        p, t = j // tiles, j % tiles
+        amps = amps + dot(both(panel[j]), fpair[p, :, t * LANES:(t + 1) * LANES], NT)
+    amps = quarters(amps)
+    for s in range(subs):
+        out_h[:, s, :] = twice(amps, pair[:, s * width:(s + 1) * width])
+
+    landed(fcat.at[pl.ds(0, moved), :], f_ssem)
+
+    @pl.when(is_head)
+    def _():
+        landed(c_recv.at[pl.ds(0, 3)], c_ssem)
+
+    @pl.when(jnp.logical_not(is_head))
+    def _():
+        landed(c_recv.at[pl.ds(0, 4)], c_ssem)
+        landed(factor, g_ssem)
+
+    @pl.when(is_owner)
+    def _():
+        landed(p_send.at[pl.ds(0, slabs - 1)], p_ssem)
+        for t in range(devices - 1):
+            s_copy(t).wait_send()
+
+    @pl.when(jnp.logical_and(is_head, g >= slabs))
+    def _():
+        landed(p_send, p_ssem)
+
+
+def near_body(sub_size, crs_size, mult, own, nbr, face, nlist, factor):
+    nk, subs, width = own.shape
+    nrhs = mult.shape[0]
+    cols = factor.shape[1]
+    slabs = crs_size * cols // LANES
+    f32, bf16 = jnp.float32, jnp.bfloat16
+    dma = pltpu.SemaphoreType.DMA
+    hbm = pl.BlockSpec(memory_space=pl.ANY)
+    names = nlist.T
+    applied = pl.pallas_call(
+        functools.partial(near_kernel, sub_size, crs_size),
+        out_shape=pltpu.VMEM(mult.shape, mult.dtype),
+        in_specs=[hbm] * 6,
+        out_specs=pl.BlockSpec(memory_space=pltpu.VMEM),
+        scratch_shapes=[
+            pltpu.VMEM(mult.shape, f32), pltpu.VMEM(own.shape, f32), pltpu.VMEM(nbr.shape, f32),
+            pltpu.VMEM(face.shape, face.dtype), pltpu.SMEM(names.shape, names.dtype),
+            pltpu.VMEM(factor.shape, f32),
+            pltpu.VMEM((LANES, subs * width), f32),
+            pltpu.VMEM((2 * LANES, subs * width), bf16),
+            pltpu.VMEM((nrhs, LANES), f32),
+            pltpu.VMEM((4 * crs_size, nrhs, LANES), f32),
+            pltpu.VMEM((crs_size * LANES, cols), f32),
+            pltpu.VMEM((crs_size,) + factor.shape, f32),
+            pltpu.VMEM((crs_size, 2 * LANES, cols), bf16),
+            pltpu.VMEM((crs_size, 2 * LANES, cols), bf16),
+            pltpu.VMEM((slabs, nrhs, LANES), f32),
+            pltpu.VMEM((sub_size, nrhs, LANES), f32),
+            pltpu.VMEM((nrhs, LANES), f32),
+            pltpu.VMEM((slabs, nrhs, LANES), f32),
+            dma((6,)), dma, dma, dma, dma, dma, dma, dma, dma, dma, dma,
+        ],
+        compiler_params=pltpu.CompilerParams(collective_id=0, has_side_effects=True),
+    )(mult, own, nbr, face, names, factor)
+    return mult - applied
+
+
+def wide_kernel(
     sub_size, crs_size,
     mult_h, own_h, nbr_h, face_h, nlist_h, factor_h, out_h,
     mult, own, nbr, face, nlist, factor,
@@ -327,7 +641,7 @@
     each(devices - 1, lambda i: ag_copy(i + 1).wait_send())
 
 
-def body(sub_size, crs_size, mult, own, nbr, face, nlist, factor):
+def wide_body(sub_size, crs_size, mult, own, nbr, face, nlist, factor):
     nk, subs, width = own.shape
     nrhs = mult.shape[0]
     part = nk * subs
@@ -340,7 +654,7 @@
     hbm = pl.BlockSpec(memory_space=pl.ANY)
     names = nlist.T
     applied = pl.pallas_call(
-        functools.partial(kernel, sub_size, crs_size),
+        functools.partial(wide_kernel, sub_size, crs_size),
         out_shape=pltpu.VMEM(mult.shape, mult.dtype),
         in_specs=[hbm] * 6,
         out_specs=pl.BlockSpec(memory_space=pltpu.VMEM),
@@ -370,6 +684,14 @@
     return mult - applied
 
 
+def body(sub_size, crs_size, mult, own, nbr, face, nlist, factor):
+    part = own.shape[0] * own.shape[1]
+    slabs = crs_size * factor.shape[1] // LANES
+    fits = part * crs_size <= LANES and slabs <= sub_size and factor.shape[1] % LANES == 0
+    form = near_body if fits else wide_body
+    return form(sub_size, crs_size, mult, own, nbr, face, nlist, factor)
+
+
 def solution(mesh):
     placed = (
         P(None, ("sub", "crs"), None),

time: 21.6 us -> 17.7 us (0.82)
  Pallas kernels: 20.8 us -> 16.9 us
    pallas_call x1, Pallas kernels: 20.8 us -> 16.9 us  [near_body(): pl.pallas_call(functools.partial(near_kernel, sub_size, crs_size), out_sh...]
where the time goes in v1:
time: 17.7 us; the launch traced here: 17.6 us
  Pallas kernels  16.9 us (95%)
  other arithmetic  0.69 us (4%)
    pallas_call x1, Pallas kernels, near_body(): pl.pallas_call(functools.partial(near_kernel, sub_size, crs_size), out_sh...  16.9 us
    sub x1, other arithmetic, near_body(): return mult - applied  0.69 us

profile of v1, /device:TPU:0, one launch (start us, length us, event | category | flops | bytes accessed | tf_op | source)
XLA Modules:
  0.0 17.6 jit_solution(4261568222093624770)
XLA Ops:
  0.0 0.0 copy-start
  0.0 16.9 %shard_map.64 = f32[16,4,512]{2,1,0:T(4,128)S(1)} custom-call(f32[16,4,512]{2,1,0:T(4,128)} %mult_h.1, f32[6,4,512]{2,1,0:T(4,128)} %own_h.1, f32[6,4,512]{2,1,0:T(4,128)} %nbr_h.1, s32[4,512]{1,0:T(4,128)} %face_h.1, s32[6,128]{1,0:T(8,128)} %bitcast.1, f32[48,384]{1,0:T(8,128)} %factor_h.1), custom_call_target="tpu_custom_call" | custom-call | tf_op jit(solution)/shard_map/pallas_call | solution.py:340
  16.9 0.0 copy-done
  16.9 0.7 %sub.3 = f32[16,4,512]{2,1,0:T(4,128)} subtract(f32[16,4,512]{2,1,0:T(4,128)S(1)} %copy-done, f32[16,4,512]{2,1,0:T(4,128)S(1)} %shard_map.64) | non-fusion elementwise | flops 32768 | bytes 393216 | tf_op jit(solution)/shard_map/sub | solution.py:365
Async XLA Ops:
  0.0 16.9 %copy-start = (f32[16,4,512]{2,1,0:T(4,128)S(1)}, f32[16,4,512]{2,1,0:T(4,128)}, u32[]{:S(2)}) copy-start(f32[16,4,512]{2,1,0:T(4,128)} %mult_h.1) | copy-start | bytes 393220

commit v2 on v0

--- a/solution.py
+++ b/solution.py
@@ -51,7 +51,290 @@
     return halves(dot(wide, right, NN))
 
 
-def kernel(
+def homes_of(sub_size, slabs):
+    return [sub_size // 2 - slabs // 2 + j for j in range(slabs)]
+
+
+def parted(value):
+    high = value.astype(jnp.bfloat16).astype(jnp.float32)
+    return high, value - high
+
+
+def near_kernel(
+    sub_size, crs_size,
+    mult_h, own_h, nbr_h, face_h, nlist_h, factor_h, out_h,
+    mult, own, nbr, face, nlist, factor,
+    modes, pair, s_send, s_recv, slab, high, low, a_send, a_recv,
+    in_sem, f_ssem, f_rsem, s_ssem, s_rsem, a_ssem, a_rsem,
+):
+    nk, subs, width = own.shape
+    nrhs = mult.shape[0]
+    nface = nlist.shape[0]
+    part = nk * subs
+    held = part * crs_size
+    tiles = factor.shape[1] // LANES
+    slabs = crs_size * tiles
+    row_len = sub_size // 2
+    group = subs * crs_size
+    devices = sub_size * crs_size
+    head = crs_size - 1
+    homes = homes_of(sub_size, slabs)
+    g = lax.axis_index("sub")
+    c = lax.axis_index("crs")
+    me = g * crs_size + c
+    owns = jnp.full((), False)
+    mine = jnp.zeros((), jnp.int32)
+    for j, home in enumerate(homes):
+        owns = jnp.logical_or(owns, g == home)
+        mine = jnp.where(g == home, j, mine)
+    is_owner = jnp.logical_and(c == head, owns)
+    is_plain = jnp.logical_not(is_owner)
+    keeps = jnp.logical_and(is_owner, mine >= head * tiles)
+    up, down = part, part + EDGE
+    off_x = part + 2 * EDGE
+    off_n, off_p = off_x + part, off_x + 2 * part
+    edge = off_p + part
+
+    def around(g):
+        first, second = g // row_len, g % row_len
+        return (
+            (first + 1) % 2 * row_len + second,
+            first * row_len + (second + 1) % row_len,
+            first * row_len + (second + row_len - 1) % row_len,
+        )
+
+    def landed(ref, semaphore):
+        pltpu.make_async_copy(ref, ref, semaphore).wait()
+
+    barrier = pltpu.get_barrier_semaphore()
+
+    @pl.when(is_owner)
+    def _():
+        for i in range(1, devices):
+            to = lax.rem(me + i, devices)
+            pl.semaphore_signal(
+                barrier, inc=1, device_id=(to // crs_size, lax.rem(to, crs_size)), device_id_type=MESH)
+
+    loads = [
+        pltpu.make_async_copy(a, b, in_sem.at[i]) for i, (a, b) in enumerate((
+            (factor_h, factor), (nlist_h, nlist), (face_h, face), (nbr_h, nbr), (own_h, own),
+            (mult_h, mult)))
+    ]
+    for load in loads:
+        load.start()
+    modes[...] = jnp.zeros_like(modes)
+    loads[0].wait()
+
+    @pl.when(is_owner)
+    def _():
+        pl.semaphore_wait(barrier, slabs - 1)
+
+    @pl.when(is_plain)
+    def _():
+        pl.semaphore_wait(barrier, slabs)
+
+    def f_copy(t, home):
+        return pltpu.make_async_remote_copy(
+            src_ref=factor.at[:, t * LANES:(t + 1) * LANES],
+            dst_ref=slab.at[pl.ds(pl.multiple_of(g * held, 8), held), :],
+            send_sem=f_ssem, recv_sem=f_rsem,
+            device_id=(home, head), device_id_type=MESH)
+
+    for t in range(tiles):
+        home = jnp.zeros((), jnp.int32)
+        for p in range(crs_size):
+            home = jnp.where(c == p, homes[p * tiles + t], home)
+        self_kept = jnp.logical_and(c == head, g == home)
+
+        @pl.when(jnp.logical_not(self_kept))
+        def _():
+            f_copy(t, home).start()
+
+        @pl.when(self_kept)
+        def _():
+            slab[pl.ds(pl.multiple_of(g * held, 8), held), :] = factor[:, t * LANES:(t + 1) * LANES]
+
+    for load in loads[1:5]:
+        load.wait()
+    across, after, before = around(g)
+    fc = face[...]
+    first_sub = me * subs
+    line = lax.broadcasted_iota(jnp.int32, (subs, width), 0)
+    target = jnp.zeros((subs, width), jnp.int32)
+    for f in range(nface):
+        name = jnp.zeros((subs, width), jnp.int32)
+        for s in range(subs):
+            name = jnp.where(line == s, nlist[f, first_sub + s], name)
+        target = jnp.where(fc == f, name, target)
+    third = c * subs + line
+    nxt = jnp.where(third == group - 1, 0, third + 1)
+    prv = jnp.where(third == 0, group - 1, third - 1)
+
+    def chosen(block, line):
+        return jnp.where(target == block * group + line, 1.0, 0.0)
+
+    masks = (
+        chosen(g, nxt), chosen(g, prv),
+        chosen(across, third), chosen(after, third), chosen(before, third),
+    )
+    for s in range(subs):
+        at = pl.ds(s * width, width)
+        own_s = own[:, s, :]
+        nbr_s = nbr[:, s, :]
+        rows = (
+            nk * (s + 1) if s < subs - 1 else up,
+            nk * (s - 1) if s > 0 else down + EDGE - nk,
+            off_x + nk * s, off_n + nk * s, off_p + nk * s,
+        )
+        modes[pl.ds(nk * s, nk), at] = own_s
+        for d in range(5):
+            modes[pl.ds(rows[d], nk), at] = nbr_s * masks[d][s:s + 1, :]
+    loads[5].wait()
+    sums = jnp.zeros((2 * nrhs, 2 * LANES), jnp.float32)
+    for s in range(subs):
+        at = pl.ds(s * width, width)
+        split = both(modes[:, at])
+        pair[:, at] = split
+        sums = sums + dot(both(mult[:, s, :]), split, NT)
+    sums = quarters(sums)
+    s_send[...] = sums
+
+    def s_copy(j):
+        return pltpu.make_async_remote_copy(
+            src_ref=s_send, dst_ref=s_recv.at[me],
+            send_sem=s_ssem, recv_sem=s_rsem,
+            device_id=(homes[j], head), device_id_type=MESH)
+
+    for j in range(slabs):
+        @pl.when(jnp.logical_not(jnp.logical_and(is_owner, mine == j)))
+        def _():
+            s_copy(j).start()
+
+    spare = jnp.zeros((LANES - edge, LANES), jnp.float32)
+
+    def rows_of(ref, d):
+        b, p = d // crs_size, d % crs_size
+
+        def take(block, p, start=0, size=part):
+            at = block * held + p * part + start
+            return ref[at:at + size, :]
+
+        x, n, q = around(b)
+        return jnp.concatenate([
+            take(b, p), take(b, (p + 1) % crs_size, 0, EDGE),
+            take(b, (p - 1) % crs_size, part - EDGE, EDGE),
+            take(x, p), take(n, p), take(q, p), spare], axis=0)
+
+    def tile_of(k):
+        return jnp.concatenate([
+            jnp.concatenate([rows_of(high, d), rows_of(low, d)], axis=1)
+            for d in (2 * k, 2 * k + 1)], axis=0)
+
+    def a_copy(d):
+        return pltpu.make_async_remote_copy(
+            src_ref=a_send.at[d], dst_ref=a_recv.at[mine],
+            send_sem=a_ssem, recv_sem=a_rsem,
+            device_id=(d // crs_size, d % crs_size), device_id_type=MESH)
+
+    @pl.when(is_owner)
+    def _():
+        s_recv[me] = sums
+
+        @pl.when(keeps)
+        def _():
+            landed(slab.at[pl.ds(0, (sub_size - 1) * held), :], f_rsem)
+
+        @pl.when(jnp.logical_not(keeps))
+        def _():
+            landed(slab, f_rsem)
+
+        high[...], low[...] = parted(slab[...])
+        landed(s_recv.at[pl.ds(0, devices - 1)], s_rsem)
+        total = jnp.zeros((2 * nrhs, 2 * LANES), jnp.float32)
+        for k in range(devices // 2):
+            both_sums = jnp.concatenate([s_recv[2 * k], s_recv[2 * k + 1]], axis=1)
+            total = total + dot(jnp.concatenate(parted(both_sums), axis=0), tile_of(k), NN)
+        panel = quarters(total)
+        ph, pw = parted(panel)
+        wide = jnp.concatenate(
+            [jnp.concatenate([ph, ph], axis=1), jnp.concatenate([pw, pw], axis=1)], axis=0)
+        for k in range(devices // 2):
+            term = halves(dot(wide, tile_of(k), NT))
+            for i in range(2):
+                d = 2 * k + i
+                a_send[d] = term[:, i * LANES:(i + 1) * LANES]
+
+                @pl.when(me != d)
+                def _():
+                    a_copy(d).start()
+        a_recv[mine] = a_send[me]
+        landed(a_recv.at[pl.ds(0, slabs - 1)], a_rsem)
+
+    @pl.when(is_plain)
+    def _():
+        landed(a_recv, a_rsem)
+
+    amps = a_recv[0]
+    for j in range(1, slabs):
+        amps = amps + a_recv[j]
+    for s in range(subs):
+        out_h[:, s, :] = twice(amps, pair[:, s * width:(s + 1) * width])
+
+    @pl.when(keeps)
+    def _():
+        landed(factor.at[:, 0:(tiles - 1) * LANES], f_ssem)
+
+    @pl.when(jnp.logical_not(keeps))
+    def _():
+        landed(factor, f_ssem)
+
+    @pl.when(is_owner)
+    def _():
+        landed(s_recv.at[pl.ds(0, slabs - 1)], s_ssem)
+        landed(a_send.at[pl.ds(0, devices - 1)], a_ssem)
+
+    @pl.when(is_plain)
+    def _():
+        landed(s_recv.at[pl.ds(0, slabs)], s_ssem)
+
+
+def near_body(sub_size, crs_size, mult, own, nbr, face, nlist, factor):
+    nk, subs, width = own.shape
+    nrhs = mult.shape[0]
+    cols = factor.shape[1]
+    devices = sub_size * crs_size
+    slabs = crs_size * cols // LANES
+    order = sub_size * factor.shape[0]
+    f32, bf16 = jnp.float32, jnp.bfloat16
+    dma = pltpu.SemaphoreType.DMA
+    hbm = pl.BlockSpec(memory_space=pl.ANY)
+    names = nlist.T
+    applied = pl.pallas_call(
+        functools.partial(near_kernel, sub_size, crs_size),
+        out_shape=pltpu.VMEM(mult.shape, mult.dtype),
+        in_specs=[hbm] * 6,
+        out_specs=pl.BlockSpec(memory_space=pltpu.VMEM),
+        scratch_shapes=[
+            pltpu.VMEM(mult.shape, f32), pltpu.VMEM(own.shape, f32), pltpu.VMEM(nbr.shape, f32),
+            pltpu.VMEM(face.shape, face.dtype), pltpu.SMEM(names.shape, names.dtype),
+            pltpu.VMEM(factor.shape, f32),
+            pltpu.VMEM((LANES, subs * width), f32),
+            pltpu.VMEM((2 * LANES, subs * width), bf16),
+            pltpu.VMEM((nrhs, LANES), f32),
+            pltpu.VMEM((devices, nrhs, LANES), f32),
+            pltpu.VMEM((order, LANES), f32),
+            pltpu.VMEM((order, LANES), f32),
+            pltpu.VMEM((order, LANES), f32),
+            pltpu.VMEM((devices, nrhs, LANES), f32),
+            pltpu.VMEM((slabs, nrhs, LANES), f32),
+            dma((6,)), dma, dma, dma, dma, dma, dma,
+        ],
+        compiler_params=pltpu.CompilerParams(collective_id=0, has_side_effects=True),
+    )(mult, own, nbr, face, names, factor)
+    return mult - applied
+
+
+def wide_kernel(
     sub_size, crs_size,
     mult_h, own_h, nbr_h, face_h, nlist_h, factor_h, out_h,
     mult, own, nbr, face, nlist, factor,
@@ -327,7 +610,7 @@
     each(devices - 1, lambda i: ag_copy(i + 1).wait_send())
 
 
-def body(sub_size, crs_size, mult, own, nbr, face, nlist, factor):
+def wide_body(sub_size, crs_size, mult, own, nbr, face, nlist, factor):
     nk, subs, width = own.shape
     nrhs = mult.shape[0]
     part = nk * subs
@@ -340,7 +623,7 @@
     hbm = pl.BlockSpec(memory_space=pl.ANY)
     names = nlist.T
     applied = pl.pallas_call(
-        functools.partial(kernel, sub_size, crs_size),
+        functools.partial(wide_kernel, sub_size, crs_size),
         out_shape=pltpu.VMEM(mult.shape, mult.dtype),
         in_specs=[hbm] * 6,
         out_specs=pl.BlockSpec(memory_space=pltpu.VMEM),
@@ -370,6 +653,13 @@
     return mult - applied
 
 
+def body(sub_size, crs_size, mult, own, nbr, face, nlist, factor):
+    slabs = crs_size * factor.shape[1] // LANES
+    fits = slabs <= sub_size // 2 and factor.shape[1] % LANES == 0 and sub_size * crs_size <= LANES // 2
+    form = near_body if fits else wide_body
+    return form(sub_size, crs_size, mult, own, nbr, face, nlist, factor)
+
+
 def solution(mesh):
     placed = (
         P(None, ("sub", "crs"), None),

time: 21.6 us -> 15.9 us (0.74)
  Pallas kernels: 20.8 us -> 15.1 us
    pallas_call x1, Pallas kernels: 20.8 us -> 15.1 us  [near_body(): pl.pallas_call(functools.partial(near_kernel, sub_size, crs_size), out_sh...]
where the time goes in v2:
time: 15.9 us; the launch traced here: 15.8 us
  Pallas kernels  15.1 us (95%)
  other arithmetic  0.69 us (4%)
    pallas_call x1, Pallas kernels, near_body(): pl.pallas_call(functools.partial(near_kernel, sub_size, crs_size), out_sh...  15.1 us
    sub x1, other arithmetic, near_body(): return mult - applied  0.69 us

profile of v2, /device:TPU:0, one launch (start us, length us, event | category | flops | bytes accessed | tf_op | source)
XLA Modules:
  0.0 15.8 jit_solution(5401202680332627830)
XLA Ops:
  0.0 0.0 copy-start
  0.0 15.1 %shard_map.64 = f32[16,4,512]{2,1,0:T(4,128)S(1)} custom-call(f32[16,4,512]{2,1,0:T(4,128)} %mult_h.1, f32[6,4,512]{2,1,0:T(4,128)} %own_h.1, f32[6,4,512]{2,1,0:T(4,128)} %nbr_h.1, s32[4,512]{1,0:T(4,128)} %face_h.1, s32[6,128]{1,0:T(8,128)} %bitcast.1, f32[48,384]{1,0:T(8,128)} %factor_h.1), custom_call_target="tpu_custom_call" | custom-call | tf_op jit(solution)/shard_map/pallas_call | solution.py:312
  15.1 0.0 copy-done
  15.1 0.7 %sub.3 = f32[16,4,512]{2,1,0:T(4,128)} subtract(f32[16,4,512]{2,1,0:T(4,128)S(1)} %copy-done, f32[16,4,512]{2,1,0:T(4,128)S(1)} %shard_map.64) | non-fusion elementwise | flops 32768 | bytes 393216 | tf_op jit(solution)/shard_map/sub | solution.py:334
Async XLA Ops:
  0.0 15.1 %copy-start = (f32[16,4,512]{2,1,0:T(4,128)S(1)}, f32[16,4,512]{2,1,0:T(4,128)}, u32[]{:S(2)}) copy-start(f32[16,4,512]{2,1,0:T(4,128)} %mult_h.1) | copy-start | bytes 393220

commit v3 on v2

--- a/solution.py
+++ b/solution.py
@@ -52,7 +52,8 @@
 
 
 def homes_of(sub_size, slabs):
-    return [sub_size // 2 - slabs // 2 + j for j in range(slabs)]
+    q = sub_size // 4
+    return (1, 2 * q, q + 1, q, q + 2, 2 * q + 2)[:slabs]
 
 
 def parted(value):
@@ -110,8 +111,8 @@
 
     @pl.when(is_owner)
     def _():
-        for i in range(1, devices):
-            to = lax.rem(me + i, devices)
+        for i in range(devices - 1):
+            to = i + jnp.where(i >= me, 1, 0)
             pl.semaphore_signal(
                 barrier, inc=1, device_id=(to // crs_size, lax.rem(to, crs_size)), device_id_type=MESH)
 
@@ -133,17 +134,25 @@
     def _():
         pl.semaphore_wait(barrier, slabs)
 
+    def home_of(j):
+        home = jnp.zeros((), jnp.int32)
+        for i in range(slabs):
+            home = jnp.where(j == i, homes[i], home)
+        return home
+
+    def tile_in(t):
+        return factor.at[:, pl.ds(pl.multiple_of(t * LANES, LANES), LANES)]
+
     def f_copy(t, home):
         return pltpu.make_async_remote_copy(
-            src_ref=factor.at[:, t * LANES:(t + 1) * LANES],
+            src_ref=tile_in(t),
             dst_ref=slab.at[pl.ds(pl.multiple_of(g * held, 8), held), :],
             send_sem=f_ssem, recv_sem=f_rsem,
             device_id=(home, head), device_id_type=MESH)
 
     for t in range(tiles):
-        home = jnp.zeros((), jnp.int32)
-        for p in range(crs_size):
-            home = jnp.where(c == p, homes[p * tiles + t], home)
+        t = lax.rem(t + g, tiles)
+        home = home_of(c * tiles + t)
         self_kept = jnp.logical_and(c == head, g == home)
 
         @pl.when(jnp.logical_not(self_kept))
@@ -152,7 +161,7 @@
 
         @pl.when(self_kept)
         def _():
-            slab[pl.ds(pl.multiple_of(g * held, 8), held), :] = factor[:, t * LANES:(t + 1) * LANES]
+            slab[pl.ds(pl.multiple_of(g * held, 8), held), :] = tile_in(t)[...]
 
     for load in loads[1:5]:
         load.wait()
@@ -203,12 +212,14 @@
         return pltpu.make_async_remote_copy(
             src_ref=s_send, dst_ref=s_recv.at[me],
             send_sem=s_ssem, recv_sem=s_rsem,
-            device_id=(homes[j], head), device_id_type=MESH)
-
-    for j in range(slabs):
-        @pl.when(jnp.logical_not(jnp.logical_and(is_owner, mine == j)))
-        def _():
-            s_copy(j).start()
+            device_id=(home_of(j), head), device_id_type=MESH)
+
+    for j in range(slabs - 1):
+        s_copy(j + jnp.where(jnp.logical_and(is_owner, j >= mine), 1, 0)).start()
+
+    @pl.when(is_plain)
+    def _():
+        s_copy(slabs - 1).start()
 
     spare = jnp.zeros((LANES - edge, LANES), jnp.float32)
 
@@ -234,7 +245,16 @@
         return pltpu.make_async_remote_copy(
             src_ref=a_send.at[d], dst_ref=a_recv.at[mine],
             send_sem=a_ssem, recv_sem=a_rsem,
-            device_id=(d // crs_size, d % crs_size), device_id_type=MESH)
+            device_id=(lax.div(d, crs_size), lax.rem(d, crs_size)), device_id_type=MESH)
+
+    def a_group(start, stop):
+        inside = jnp.logical_and(me >= start, me < stop)
+        for d in range(start, stop - 1):
+            a_copy(d + jnp.where(jnp.logical_and(inside, d >= me), 1, 0)).start()
+
+        @pl.when(jnp.logical_not(inside))
+        def _():
+            a_copy(jnp.int32(stop - 1)).start()
 
     @pl.when(is_owner)
     def _():
@@ -258,15 +278,16 @@
         ph, pw = parted(panel)
         wide = jnp.concatenate(
             [jnp.concatenate([ph, ph], axis=1), jnp.concatenate([pw, pw], axis=1)], axis=0)
-        for k in range(devices // 2):
+        def form(k):
             term = halves(dot(wide, tile_of(k), NT))
             for i in range(2):
-                d = 2 * k + i
-                a_send[d] = term[:, i * LANES:(i + 1) * LANES]
-
-                @pl.when(me != d)
-                def _():
-                    a_copy(d).start()
+                a_send[2 * k + i] = term[:, i * LANES:(i + 1) * LANES]
+
+        quarter = devices // 4
+        for start, stop in ((0, 2), (3 * quarter, devices), (2 * quarter, 3 * quarter), (2, quarter), (quarter, 2 * quarter)):
+            for k in range(start // 2, stop // 2):
+                form(k)
+            a_group(start, stop)
         a_recv[mine] = a_send[me]
         landed(a_recv.at[pl.ds(0, slabs - 1)], a_rsem)
 
@@ -655,7 +676,7 @@
 
 def body(sub_size, crs_size, mult, own, nbr, face, nlist, factor):
     slabs = crs_size * factor.shape[1] // LANES
-    fits = slabs <= sub_size // 2 and factor.shape[1] % LANES == 0 and sub_size * crs_size <= LANES // 2
+    fits = slabs <= 6 and factor.shape[1] % LANES == 0 and 12 <= sub_size <= LANES // 4
     form = near_body if fits else wide_body
     return form(sub_size, crs_size, mult, own, nbr, face, nlist, factor)
 

time: 15.9 us -> 15.2 us (0.956)
  Pallas kernels: 15.1 us -> 14.3 us
    pallas_call x1, Pallas kernels: 15.1 us -> 14.3 us  [near_body(): pl.pallas_call(functools.partial(near_kernel, sub_size, crs_size), out_sh...]
where the time goes in v3:
time: 15.2 us; the launch traced here: 15 us
  Pallas kernels  14.3 us (94%)
  other arithmetic  0.69 us (5%)
    pallas_call x1, Pallas kernels, near_body(): pl.pallas_call(functools.partial(near_kernel, sub_size, crs_size), out_sh...  14.3 us
    sub x1, other arithmetic, near_body(): return mult - applied  0.69 us

profile of v3, /device:TPU:0, one launch (start us, length us, event | category | flops | bytes accessed | tf_op | source)
XLA Modules:
  0.0 15.0 jit_solution(15809235580357369949)
XLA Ops:
  0.0 0.0 copy-start
  0.0 14.3 %shard_map.64 = f32[16,4,512]{2,1,0:T(4,128)S(1)} custom-call(f32[16,4,512]{2,1,0:T(4,128)} %mult_h.1, f32[6,4,512]{2,1,0:T(4,128)} %own_h.1, f32[6,4,512]{2,1,0:T(4,128)} %nbr_h.1, s32[4,512]{1,0:T(4,128)} %face_h.1, s32[6,128]{1,0:T(8,128)} %bitcast.1, f32[48,384]{1,0:T(8,128)} %factor_h.1), custom_call_target="tpu_custom_call" | custom-call | tf_op jit(solution)/shard_map/pallas_call | solution.py:333
  14.3 0.0 copy-done
  14.3 0.7 %sub.3 = f32[16,4,512]{2,1,0:T(4,128)} subtract(f32[16,4,512]{2,1,0:T(4,128)S(1)} %copy-done, f32[16,4,512]{2,1,0:T(4,128)S(1)} %shard_map.64) | non-fusion elementwise | flops 32768 | bytes 393216 | tf_op jit(solution)/shard_map/sub | solution.py:355
Async XLA Ops:
  0.0 14.3 %copy-start = (f32[16,4,512]{2,1,0:T(4,128)S(1)}, f32[16,4,512]{2,1,0:T(4,128)}, u32[]{:S(2)}) copy-start(f32[16,4,512]{2,1,0:T(4,128)} %mult_h.1) | copy-start | bytes 393220

commit v4 on v3

--- a/solution.py
+++ b/solution.py
@@ -53,7 +53,11 @@
 
 def homes_of(sub_size, slabs):
     q = sub_size // 4
-    return (1, 2 * q, q + 1, q, q + 2, 2 * q + 2)[:slabs]
+    return (q, 2 * q + 2, q + 2, 2 * q + 1, q + 1, 2 * q)[:slabs]
+
+
+WAVES = 4
+N2, N3 = 2, 2
 
 
 def parted(value):
@@ -65,7 +69,7 @@
     sub_size, crs_size,
     mult_h, own_h, nbr_h, face_h, nlist_h, factor_h, out_h,
     mult, own, nbr, face, nlist, factor,
-    modes, pair, s_send, s_recv, slab, high, low, a_send, a_recv,
+    modes, pair, s_send, s_recv, e_rows, slab, high, low, a_send, a_recv,
     in_sem, f_ssem, f_rsem, s_ssem, s_rsem, a_ssem, a_rsem,
 ):
     nk, subs, width = own.shape
@@ -79,6 +83,7 @@
     group = subs * crs_size
     devices = sub_size * crs_size
     head = crs_size - 1
+    wave = sub_size // WAVES
     homes = homes_of(sub_size, slabs)
     g = lax.axis_index("sub")
     c = lax.axis_index("crs")
@@ -91,10 +96,8 @@
     is_owner = jnp.logical_and(c == head, owns)
     is_plain = jnp.logical_not(is_owner)
     keeps = jnp.logical_and(is_owner, mine >= head * tiles)
-    up, down = part, part + EDGE
-    off_x = part + 2 * EDGE
-    off_n, off_p = off_x + part, off_x + 2 * part
-    edge = off_p + part
+    far = 2 * held
+    edge = far + part
 
     def around(g):
         first, second = g // row_len, g % row_len
@@ -123,16 +126,25 @@
     ]
     for load in loads:
         load.start()
-    modes[...] = jnp.zeros_like(modes)
+    modes[edge:, :] = jnp.zeros((LANES - edge, modes.shape[1]), jnp.float32)
+
+    @pl.when(is_owner)
+    def _():
+        for i in range(sub_size // 2):
+            slab[i * LANES + far:(i + 1) * LANES, :] = jnp.zeros((LANES - far, LANES), jnp.float32)
+
     loads[0].wait()
-
-    @pl.when(is_owner)
-    def _():
-        pl.semaphore_wait(barrier, slabs - 1)
-
-    @pl.when(is_plain)
-    def _():
-        pl.semaphore_wait(barrier, slabs)
+    late = g >= sub_size // 2
+    last = g >= sub_size - wave
+
+    def meet():
+        @pl.when(is_owner)
+        def _():
+            pl.semaphore_wait(barrier, slabs - 1)
+
+        @pl.when(is_plain)
+        def _():
+            pl.semaphore_wait(barrier, slabs)
 
     def home_of(j):
         home = jnp.zeros((), jnp.int32)
@@ -146,11 +158,11 @@
     def f_copy(t, home):
         return pltpu.make_async_remote_copy(
             src_ref=tile_in(t),
-            dst_ref=slab.at[pl.ds(pl.multiple_of(g * held, 8), held), :],
+            dst_ref=slab.at[pl.ds(pl.multiple_of(g // 2 * LANES + lax.rem(g, 2) * held, 8), held), :],
             send_sem=f_ssem, recv_sem=f_rsem,
             device_id=(home, head), device_id_type=MESH)
 
-    for t in range(tiles):
+    def f_start(t):
         t = lax.rem(t + g, tiles)
         home = home_of(c * tiles + t)
         self_kept = jnp.logical_and(c == head, g == home)
@@ -161,7 +173,18 @@
 
         @pl.when(self_kept)
         def _():
-            slab[pl.ds(pl.multiple_of(g * held, 8), held), :] = tile_in(t)[...]
+            slab[pl.ds(pl.multiple_of(g // 2 * LANES + lax.rem(g, 2) * held, 8), held), :] = tile_in(t)[...]
+
+    @pl.when(late)
+    def _():
+        meet()
+        for t in range(N2):
+            f_start(t)
+
+    @pl.when(last)
+    def _():
+        for t in range(N2, N3):
+            f_start(t)
 
     for load in loads[1:5]:
         load.wait()
@@ -186,18 +209,44 @@
         chosen(g, nxt), chosen(g, prv),
         chosen(across, third), chosen(after, third), chosen(before, third),
     )
+    here, there = lax.rem(g, 2) * held, lax.rem(g + 1, 2) * held
+    mine_at, other_at = c * part, (1 - c) * part
+
+    def block(*pieces):
+        rows, at = [], 0
+        for start, value in pieces:
+            if start > at:
+                rows.append(jnp.zeros((start - at, width), jnp.float32))
+            rows.append(value)
+            at = start + nk
+        if at < part:
+            rows.append(jnp.zeros((part - at, width), jnp.float32))
+        return jnp.concatenate(rows, axis=0)
+
     for s in range(subs):
-        at = pl.ds(s * width, width)
         own_s = own[:, s, :]
         nbr_s = nbr[:, s, :]
-        rows = (
-            nk * (s + 1) if s < subs - 1 else up,
-            nk * (s - 1) if s > 0 else down + EDGE - nk,
-            off_x + nk * s, off_n + nk * s, off_p + nk * s,
-        )
-        modes[pl.ds(nk * s, nk), at] = own_s
-        for d in range(5):
-            modes[pl.ds(rows[d], nk), at] = nbr_s * masks[d][s:s + 1, :]
+        to = [nbr_s * masks[d][s:s + 1, :] for d in range(5)]
+        first_at, last_at = s == 0, s == subs - 1
+        inner = [(nk * s, own_s)]
+        if not last_at:
+            inner.append((nk * (s + 1), to[0]))
+        if not first_at:
+            inner.insert(0, (nk * (s - 1), to[1]))
+        outer = []
+        if last_at:
+            outer.append((0, to[0]))
+        if first_at:
+            outer.append((part - nk, to[1]))
+        for base, value in (
+            (here + mine_at, block(*inner)),
+            (here + other_at, block(*outer)),
+            (there + mine_at, block((nk * s, to[3]))),
+            (there + other_at, block((nk * s, to[4]))),
+            (far, block((nk * s, to[2]))),
+        ):
+            start = base if isinstance(base, int) else pl.multiple_of(base, 8)
+            modes[pl.ds(start, part), pl.ds(s * width, width)] = value
     loads[5].wait()
     sums = jnp.zeros((2 * nrhs, 2 * LANES), jnp.float32)
     for s in range(subs):
@@ -207,11 +256,12 @@
         sums = sums + dot(both(mult[:, s, :]), split, NT)
     sums = quarters(sums)
     s_send[...] = sums
+    pl.when(jnp.logical_not(late))(meet)
 
     def s_copy(j):
         return pltpu.make_async_remote_copy(
             src_ref=s_send, dst_ref=s_recv.at[me],
-            send_sem=s_ssem, recv_sem=s_rsem,
+            send_sem=s_ssem, recv_sem=s_rsem.at[g // wave],
             device_id=(home_of(j), head), device_id_type=MESH)
 
     for j in range(slabs - 1):
@@ -221,25 +271,18 @@
     def _():
         s_copy(slabs - 1).start()
 
-    spare = jnp.zeros((LANES - edge, LANES), jnp.float32)
-
-    def rows_of(ref, d):
-        b, p = d // crs_size, d % crs_size
-
-        def take(block, p, start=0, size=part):
-            at = block * held + p * part + start
-            return ref[at:at + size, :]
-
-        x, n, q = around(b)
-        return jnp.concatenate([
-            take(b, p), take(b, (p + 1) % crs_size, 0, EDGE),
-            take(b, (p - 1) % crs_size, part - EDGE, EDGE),
-            take(x, p), take(n, p), take(q, p), spare], axis=0)
-
-    def tile_of(k):
-        return jnp.concatenate([
-            jnp.concatenate([rows_of(high, d), rows_of(low, d)], axis=1)
-            for d in (2 * k, 2 * k + 1)], axis=0)
+    @pl.when(jnp.logical_not(late))
+    def _():
+        for t in range(N2):
+            f_start(t)
+
+    @pl.when(jnp.logical_not(last))
+    def _():
+        for t in range(N2, N3):
+            f_start(t)
+
+    for t in range(N3, tiles):
+        f_start(t)
 
     def a_copy(d):
         return pltpu.make_async_remote_copy(
@@ -260,33 +303,94 @@
     def _():
         s_recv[me] = sums
 
-        @pl.when(keeps)
-        def _():
-            landed(slab.at[pl.ds(0, (sub_size - 1) * held), :], f_rsem)
-
-        @pl.when(jnp.logical_not(keeps))
-        def _():
-            landed(slab, f_rsem)
-
-        high[...], low[...] = parted(slab[...])
-        landed(s_recv.at[pl.ds(0, devices - 1)], s_rsem)
-        total = jnp.zeros((2 * nrhs, 2 * LANES), jnp.float32)
-        for k in range(devices // 2):
-            both_sums = jnp.concatenate([s_recv[2 * k], s_recv[2 * k + 1]], axis=1)
-            total = total + dot(jnp.concatenate(parted(both_sums), axis=0), tile_of(k), NN)
-        panel = quarters(total)
+        lane = lax.broadcasted_iota(jnp.int32, (nrhs, LANES), 1)
+        rhs = [jnp.zeros((nrhs, LANES), jnp.float32)] * (sub_size // 2)
+
+        def rows_of(d):
+            b, p = d // crs_size, d % crs_size
+            x, n, q = around(b)
+
+            def take(block, start, size):
+                at = block // 2 * LANES + block % 2 * held + start
+                return jnp.concatenate([high[at:at + size, :], low[at:at + size, :]], axis=1)
+
+            others = [take(n, p * part, part), take(q, p * part, part)]
+            halves_of = [take(b, 0, held), jnp.concatenate(others if p == 0 else others[::-1], axis=0)]
+            spare = jnp.zeros((LANES - edge, 2 * LANES), jnp.float32)
+            return jnp.concatenate(
+                (halves_of if b % 2 == 0 else halves_of[::-1]) + [take(x, p * part, part), spare], axis=0)
+
+        def only(value, at, size):
+            return jnp.where((lane >= at) & (lane < at + size), value, 0.0)
+
+        def turned(value, by):
+            return pltpu.roll(value, by % LANES, 1)
+
+        order = (*range(WAVES - 2), WAVES - 1, WAVES - 2)
+        for w in order:
+            inside = g // wave == w
+            count = wave * crs_size
+
+            @pl.when(inside)
+            def _():
+                landed(s_recv.at[pl.ds(0, count - 1)], s_rsem.at[w])
+
+            @pl.when(jnp.logical_not(inside))
+            def _():
+                landed(s_recv.at[pl.ds(0, count)], s_rsem.at[w])
+
+            for b in range(w * wave, (w + 1) * wave):
+                x, n, q = around(b)
+                this, that = b % 2 * held, (b + 1) % 2 * held
+                pair_sum = s_recv[b * crs_size] + s_recv[b * crs_size + 1]
+                rhs[b // 2] = rhs[b // 2] + only(pair_sum, this, held)
+                for p in range(crs_size):
+                    value = s_recv[b * crs_size + p]
+                    at, off = p * part, (1 - p) * part
+                    rhs[n // 2] = rhs[n // 2] + only(value, that + at, part)
+                    rhs[q // 2] = rhs[q // 2] + only(turned(value, at - off), that + at, part)
+                    rhs[x // 2] = rhs[x // 2] + only(turned(value, this + at - far), this + at, part)
+            if w == order[-2]:
+                @pl.when(keeps)
+                def _():
+                    landed(slab.at[pl.ds(0, (sub_size - 1) * held), :], f_rsem)
+
+                @pl.when(jnp.logical_not(keeps))
+                def _():
+                    landed(slab.at[pl.ds(0, sub_size * held), :], f_rsem)
+
+                high[...], low[...] = parted(slab[...])
+        for i, value in enumerate(rhs):
+            at = pl.ds(i * LANES, LANES)
+            e_rows[0:nrhs, at], e_rows[nrhs:2 * nrhs, at] = parted(value)
+        split = jnp.concatenate([high[...], low[...]], axis=1)
+        panel = quarters(dot(e_rows[...], split, NN))
         ph, pw = parted(panel)
         wide = jnp.concatenate(
             [jnp.concatenate([ph, ph], axis=1), jnp.concatenate([pw, pw], axis=1)], axis=0)
-        def form(k):
-            term = halves(dot(wide, tile_of(k), NT))
-            for i in range(2):
-                a_send[2 * k + i] = term[:, i * LANES:(i + 1) * LANES]
+        first_rows = jnp.concatenate([rows_of(d) for d in range(crs_size)], axis=0)
+        term = halves(dot(wide, first_rows, NT))
+        for d in range(crs_size):
+            a_send[d] = term[:, d * LANES:(d + 1) * LANES]
+            a_copy(jnp.int32(d)).start()
+        amps = halves(dot(wide, split, NT))
+        tiled = [amps[:, i * LANES:(i + 1) * LANES] for i in range(sub_size // 2)]
+
+        def form(d):
+            b, p = d // crs_size, d % crs_size
+            x, n, q = around(b)
+            this, that = b % 2 * held, (b + 1) % 2 * held
+            at, off = p * part, (1 - p) * part
+            value = turned(tiled[x // 2], far - this - at)
+            value = jnp.where((lane >= this) & (lane < this + held), tiled[b // 2], value)
+            value = jnp.where((lane >= that + at) & (lane < that + at + part), tiled[n // 2], value)
+            a_send[d] = jnp.where(
+                (lane >= that + off) & (lane < that + off + part), turned(tiled[q // 2], off - at), value)
 
         quarter = devices // 4
-        for start, stop in ((0, 2), (3 * quarter, devices), (2 * quarter, 3 * quarter), (2, quarter), (quarter, 2 * quarter)):
-            for k in range(start // 2, stop // 2):
-                form(k)
+        for start, stop in ((3 * quarter, devices), (2 * quarter, 3 * quarter), (2, quarter), (quarter, 2 * quarter)):
+            for d in range(start, stop):
+                form(d)
             a_group(start, stop)
         a_recv[mine] = a_send[me]
         landed(a_recv.at[pl.ds(0, slabs - 1)], a_rsem)
@@ -325,7 +429,7 @@
     cols = factor.shape[1]
     devices = sub_size * crs_size
     slabs = crs_size * cols // LANES
-    order = sub_size * factor.shape[0]
+    order = sub_size * (LANES // 2)
     f32, bf16 = jnp.float32, jnp.bfloat16
     dma = pltpu.SemaphoreType.DMA
     hbm = pl.BlockSpec(memory_space=pl.ANY)
@@ -343,12 +447,13 @@
             pltpu.VMEM((2 * LANES, subs * width), bf16),
             pltpu.VMEM((nrhs, LANES), f32),
             pltpu.VMEM((devices, nrhs, LANES), f32),
+            pltpu.VMEM((2 * nrhs, order), f32),
             pltpu.VMEM((order, LANES), f32),
             pltpu.VMEM((order, LANES), f32),
             pltpu.VMEM((order, LANES), f32),
             pltpu.VMEM((devices, nrhs, LANES), f32),
             pltpu.VMEM((slabs, nrhs, LANES), f32),
-            dma((6,)), dma, dma, dma, dma, dma, dma,
+            dma((6,)), dma, dma, dma, dma((WAVES,)), dma, dma,
         ],
         compiler_params=pltpu.CompilerParams(collective_id=0, has_side_effects=True),
     )(mult, own, nbr, face, names, factor)
@@ -676,7 +781,9 @@
 
 def body(sub_size, crs_size, mult, own, nbr, face, nlist, factor):
     slabs = crs_size * factor.shape[1] // LANES
-    fits = slabs <= 6 and factor.shape[1] % LANES == 0 and 12 <= sub_size <= LANES // 4
+    held = own.shape[0] * own.shape[1] * crs_size
+    fits = (slabs <= 6 and crs_size == 2 and factor.shape[1] % LANES == 0 and held * 5 <= LANES * 2
+            and 12 <= sub_size <= LANES // 4)
     form = near_body if fits else wide_body
     return form(sub_size, crs_size, mult, own, nbr, face, nlist, factor)
 

time: 15.2 us -> 15 us (0.987)
    pallas_call x1, Pallas kernels: 14.3 us -> 14.2 us  [near_body(): pl.pallas_call(functools.partial(near_kernel, sub_size, crs_size), out_sh...]
where the time goes in v4:
time: 15 us; the launch traced here: 14.9 us
  Pallas kernels  14.2 us (95%)
  other arithmetic  0.69 us (5%)
    pallas_call x1, Pallas kernels, near_body(): pl.pallas_call(functools.partial(near_kernel, sub_size, crs_size), out_sh...  14.2 us
    sub x1, other arithmetic, near_body(): return mult - applied  0.69 us

profile of v4, /device:TPU:0, one launch (start us, length us, event | category | flops | bytes accessed | tf_op | source)
XLA Modules:
  0.0 14.9 jit_solution(10706978573822190110)
XLA Ops:
  0.0 0.0 copy-start
  0.0 14.2 %shard_map.64 = f32[16,4,512]{2,1,0:T(4,128)S(1)} custom-call(f32[16,4,512]{2,1,0:T(4,128)} %mult_h.1, f32[6,4,512]{2,1,0:T(4,128)} %own_h.1, f32[6,4,512]{2,1,0:T(4,128)} %nbr_h.1, s32[4,512]{1,0:T(4,128)} %face_h.1, s32[6,128]{1,0:T(8,128)} %bitcast.1, f32[48,384]{1,0:T(8,128)} %factor_h.1), custom_call_target="tpu_custom_call" | custom-call | tf_op jit(solution)/shard_map/pallas_call | solution.py:437
  14.2 0.0 copy-done
  14.2 0.7 %sub.3 = f32[16,4,512]{2,1,0:T(4,128)} subtract(f32[16,4,512]{2,1,0:T(4,128)S(1)} %copy-done, f32[16,4,512]{2,1,0:T(4,128)S(1)} %shard_map.64) | non-fusion elementwise | flops 32768 | bytes 393216 | tf_op jit(solution)/shard_map/sub | solution.py:460
Async XLA Ops:
  0.0 14.2 %copy-start = (f32[16,4,512]{2,1,0:T(4,128)S(1)}, f32[16,4,512]{2,1,0:T(4,128)}, u32[]{:S(2)}) copy-start(f32[16,4,512]{2,1,0:T(4,128)} %mult_h.1) | copy-start | bytes 393220

commit v5 on v4

--- a/solution.py
+++ b/solution.py
@@ -56,7 +56,6 @@
     return (q, 2 * q + 2, q + 2, 2 * q + 1, q + 1, 2 * q)[:slabs]
 
 
-WAVES = 4
 N2, N3 = 2, 2
 
 
@@ -83,7 +82,6 @@
     group = subs * crs_size
     devices = sub_size * crs_size
     head = crs_size - 1
-    wave = sub_size // WAVES
     homes = homes_of(sub_size, slabs)
     g = lax.axis_index("sub")
     c = lax.axis_index("crs")
@@ -120,9 +118,9 @@
                 barrier, inc=1, device_id=(to // crs_size, lax.rem(to, crs_size)), device_id_type=MESH)
 
     loads = [
-        pltpu.make_async_copy(a, b, in_sem.at[i]) for i, (a, b) in enumerate((
-            (factor_h, factor), (nlist_h, nlist), (face_h, face), (nbr_h, nbr), (own_h, own),
-            (mult_h, mult)))
+        pltpu.make_async_copy(a, b, in_sem.at[i]) for i, a, b in (
+            (0, factor_h, factor), (1, nlist_h, nlist), (2, face_h, face), (2, nbr_h, nbr),
+            (2, own_h, own), (3, mult_h, mult))
     ]
     for load in loads:
         load.start()
@@ -135,7 +133,7 @@
 
     loads[0].wait()
     late = g >= sub_size // 2
-    last = g >= sub_size - wave
+    last = g >= sub_size - sub_size // 4
 
     def meet():
         @pl.when(is_owner)
@@ -186,8 +184,8 @@
         for t in range(N2, N3):
             f_start(t)
 
-    for load in loads[1:5]:
-        load.wait()
+    loads[1].wait()
+    landed(mult.at[pl.ds(0, 2 * nk + 1)], in_sem.at[2])
     across, after, before = around(g)
     fc = face[...]
     first_sub = me * subs
@@ -261,15 +259,16 @@
     def s_copy(j):
         return pltpu.make_async_remote_copy(
             src_ref=s_send, dst_ref=s_recv.at[me],
-            send_sem=s_ssem, recv_sem=s_rsem.at[g // wave],
+            send_sem=s_ssem, recv_sem=s_rsem,
             device_id=(home_of(j), head), device_id_type=MESH)
 
-    for j in range(slabs - 1):
-        s_copy(j + jnp.where(jnp.logical_and(is_owner, j >= mine), 1, 0)).start()
+    turn = jnp.where(is_owner, mine + 1, lax.rem(g, 2) * crs_size)
+    for i in range(slabs - 1):
+        s_copy(lax.rem(turn + i, slabs)).start()
 
     @pl.when(is_plain)
     def _():
-        s_copy(slabs - 1).start()
+        s_copy(lax.rem(turn + slabs - 1, slabs)).start()
 
     @pl.when(jnp.logical_not(late))
     def _():
@@ -326,40 +325,27 @@
         def turned(value, by):
             return pltpu.roll(value, by % LANES, 1)
 
-        order = (*range(WAVES - 2), WAVES - 1, WAVES - 2)
-        for w in order:
-            inside = g // wave == w
-            count = wave * crs_size
-
-            @pl.when(inside)
-            def _():
-                landed(s_recv.at[pl.ds(0, count - 1)], s_rsem.at[w])
-
-            @pl.when(jnp.logical_not(inside))
-            def _():
-                landed(s_recv.at[pl.ds(0, count)], s_rsem.at[w])
-
-            for b in range(w * wave, (w + 1) * wave):
-                x, n, q = around(b)
-                this, that = b % 2 * held, (b + 1) % 2 * held
-                pair_sum = s_recv[b * crs_size] + s_recv[b * crs_size + 1]
-                rhs[b // 2] = rhs[b // 2] + only(pair_sum, this, held)
-                for p in range(crs_size):
-                    value = s_recv[b * crs_size + p]
-                    at, off = p * part, (1 - p) * part
-                    rhs[n // 2] = rhs[n // 2] + only(value, that + at, part)
-                    rhs[q // 2] = rhs[q // 2] + only(turned(value, at - off), that + at, part)
-                    rhs[x // 2] = rhs[x // 2] + only(turned(value, this + at - far), this + at, part)
-            if w == order[-2]:
-                @pl.when(keeps)
-                def _():
-                    landed(slab.at[pl.ds(0, (sub_size - 1) * held), :], f_rsem)
-
-                @pl.when(jnp.logical_not(keeps))
-                def _():
-                    landed(slab.at[pl.ds(0, sub_size * held), :], f_rsem)
-
-                high[...], low[...] = parted(slab[...])
+        @pl.when(keeps)
+        def _():
+            landed(slab.at[pl.ds(0, (sub_size - 1) * held), :], f_rsem)
+
+        @pl.when(jnp.logical_not(keeps))
+        def _():
+            landed(slab.at[pl.ds(0, sub_size * held), :], f_rsem)
+
+        high[...], low[...] = parted(slab[...])
+        landed(s_recv.at[pl.ds(0, devices - 1)], s_rsem)
+        for b in range(sub_size):
+            x, n, q = around(b)
+            this, that = b % 2 * held, (b + 1) % 2 * held
+            pair_sum = s_recv[b * crs_size] + s_recv[b * crs_size + 1]
+            rhs[b // 2] = rhs[b // 2] + only(pair_sum, this, held)
+            for p in range(crs_size):
+                value = s_recv[b * crs_size + p]
+                at, off = p * part, (1 - p) * part
+                rhs[n // 2] = rhs[n // 2] + only(value, that + at, part)
+                rhs[q // 2] = rhs[q // 2] + only(turned(value, at - off), that + at, part)
+                rhs[x // 2] = rhs[x // 2] + only(turned(value, this + at - far), this + at, part)
         for i, value in enumerate(rhs):
             at = pl.ds(i * LANES, LANES)
             e_rows[0:nrhs, at], e_rows[nrhs:2 * nrhs, at] = parted(value)
@@ -403,7 +389,7 @@
     for j in range(1, slabs):
         amps = amps + a_recv[j]
     for s in range(subs):
-        out_h[:, s, :] = twice(amps, pair[:, s * width:(s + 1) * width])
+        out_h[:, s, :] = mult[:, s, :] - twice(amps, pair[:, s * width:(s + 1) * width])
 
     @pl.when(keeps)
     def _():
@@ -434,7 +420,7 @@
     dma = pltpu.SemaphoreType.DMA
     hbm = pl.BlockSpec(memory_space=pl.ANY)
     names = nlist.T
-    applied = pl.pallas_call(
+    projected = pl.pallas_call(
         functools.partial(near_kernel, sub_size, crs_size),
         out_shape=pltpu.VMEM(mult.shape, mult.dtype),
         in_specs=[hbm] * 6,
@@ -453,11 +439,11 @@
             pltpu.VMEM((order, LANES), f32),
             pltpu.VMEM((devices, nrhs, LANES), f32),
             pltpu.VMEM((slabs, nrhs, LANES), f32),
-            dma((6,)), dma, dma, dma, dma((WAVES,)), dma, dma,
+            dma((4,)), dma, dma, dma, dma, dma, dma,
         ],
         compiler_params=pltpu.CompilerParams(collective_id=0, has_side_effects=True),
     )(mult, own, nbr, face, names, factor)
-    return mult - applied
+    return projected
 
 
 def wide_kernel(
@@ -783,7 +769,7 @@
     slabs = crs_size * factor.shape[1] // LANES
     held = own.shape[0] * own.shape[1] * crs_size
     fits = (slabs <= 6 and crs_size == 2 and factor.shape[1] % LANES == 0 and held * 5 <= LANES * 2
-            and 12 <= sub_size <= LANES // 4)
+            and 12 <= sub_size <= LANES // 4 and mult.shape[0] > 2 * own.shape[0])
     form = near_body if fits else wide_body
     return form(sub_size, crs_size, mult, own, nbr, face, nlist, factor)
 

time: 15 us -> 14.8 us (0.987)
  other arithmetic: 0.69 us -> 0 us
  local copies, waits for them, and re-layouts: 0.01 us -> 0.66 us
  Pallas kernels: 14.2 us -> 14 us
    sub x1 -> x0, other arithmetic: 0.69 us -> none  [near_body(): return mult - applied]
    unnamed x2 -> x1, local copies, waits for them, and re-layouts: 0.01 us -> 0.66 us
    pallas_call x1, Pallas kernels: 14.2 us -> 14 us  [near_body(): pl.pallas_call(functools.partial(near_kernel, sub_size, crs_size), out_sh...]
where the time goes in v5:
time: 14.8 us; the launch traced here: 14.6 us
  Pallas kernels  14 us (95%)
  local copies, waits for them, and re-layouts  0.66 us (4%)
    pallas_call x1, Pallas kernels, near_body(): pl.pallas_call(functools.partial(near_kernel, sub_size, crs_size), out_sh...  14 us
    unnamed x1, local copies, waits for them, and re-layouts  0.66 us

profile of v5, /device:TPU:0, one launch (start us, length us, event | category | flops | bytes accessed | tf_op | source)
XLA Modules:
  0.0 14.6 jit_solution(5022239145395082938)
XLA Ops:
  0.0 14.0 %shard_map.64 = f32[16,4,512]{2,1,0:T(4,128)S(1)} custom-call(f32[16,4,512]{2,1,0:T(4,128)} %mult_h.1, f32[6,4,512]{2,1,0:T(4,128)} %own_h.1, f32[6,4,512]{2,1,0:T(4,128)} %nbr_h.1, s32[4,512]{1,0:T(4,128)} %face_h.1, s32[6,128]{1,0:T(8,128)} %bitcast.1, f32[48,384]{1,0:T(8,128)} %factor_h.1), custom_call_target="tpu_custom_call" | custom-call | tf_op jit(solution)/shard_map/pallas_call | solution.py:423
  14.0 0.7 %copy.8 = f32[16,4,512]{2,1,0:T(4,128)} copy(f32[16,4,512]{2,1,0:T(4,128)S(1)} %shard_map.64) | data formatting | bytes 262144

commit v6 on v5

--- a/solution.py
+++ b/solution.py
@@ -68,7 +68,7 @@
     sub_size, crs_size,
     mult_h, own_h, nbr_h, face_h, nlist_h, factor_h, out_h,
     mult, own, nbr, face, nlist, factor,
-    modes, pair, s_send, s_recv, e_rows, slab, high, low, a_send, a_recv,
+    modes, pair, s_send, s_recv, slab, high, low, a_send, a_recv,
     in_sem, f_ssem, f_rsem, s_ssem, s_rsem, a_ssem, a_rsem,
 ):
     nk, subs, width = own.shape
@@ -346,11 +346,9 @@
                 rhs[n // 2] = rhs[n // 2] + only(value, that + at, part)
                 rhs[q // 2] = rhs[q // 2] + only(turned(value, at - off), that + at, part)
                 rhs[x // 2] = rhs[x // 2] + only(turned(value, this + at - far), this + at, part)
-        for i, value in enumerate(rhs):
-            at = pl.ds(i * LANES, LANES)
-            e_rows[0:nrhs, at], e_rows[nrhs:2 * nrhs, at] = parted(value)
+        rhs_rows = jnp.concatenate(parted(jnp.concatenate(rhs, axis=1)), axis=0)
         split = jnp.concatenate([high[...], low[...]], axis=1)
-        panel = quarters(dot(e_rows[...], split, NN))
+        panel = quarters(dot(rhs_rows, split, NN))
         ph, pw = parted(panel)
         wide = jnp.concatenate(
             [jnp.concatenate([ph, ph], axis=1), jnp.concatenate([pw, pw], axis=1)], axis=0)
@@ -433,7 +431,6 @@
             pltpu.VMEM((2 * LANES, subs * width), bf16),
             pltpu.VMEM((nrhs, LANES), f32),
             pltpu.VMEM((devices, nrhs, LANES), f32),
-            pltpu.VMEM((2 * nrhs, order), f32),
             pltpu.VMEM((order, LANES), f32),
             pltpu.VMEM((order, LANES), f32),
             pltpu.VMEM((order, LANES), f32),

time: 14.8 us -> 14.8 us (level)
  no operation moved by 1% of the time
where the time goes in v6:
time: 14.8 us; the launch traced here: 14.6 us
  Pallas kernels  14 us (95%)
  local copies, waits for them, and re-layouts  0.66 us (4%)
    pallas_call x1, Pallas kernels, near_body(): pl.pallas_call(functools.partial(near_kernel, sub_size, crs_size), out_sh...  14 us
    unnamed x1, local copies, waits for them, and re-layouts  0.66 us

profile of v6, /device:TPU:0, one launch (start us, length us, event | category | flops | bytes accessed | tf_op | source)
XLA Modules:
  0.0 14.6 jit_solution(5022239145395082938)
XLA Ops:
  0.0 14.0 %shard_map.64 = f32[16,4,512]{2,1,0:T(4,128)S(1)} custom-call(f32[16,4,512]{2,1,0:T(4,128)} %mult_h.1, f32[6,4,512]{2,1,0:T(4,128)} %own_h.1, f32[6,4,512]{2,1,0:T(4,128)} %nbr_h.1, s32[4,512]{1,0:T(4,128)} %face_h.1, s32[6,128]{1,0:T(8,128)} %bitcast.1, f32[48,384]{1,0:T(8,128)} %factor_h.1), custom_call_target="tpu_custom_call" | custom-call | tf_op jit(solution)/shard_map/pallas_call | solution.py:421
  14.0 0.7 %copy.8 = f32[16,4,512]{2,1,0:T(4,128)} copy(f32[16,4,512]{2,1,0:T(4,128)S(1)} %shard_map.64) | data formatting | bytes 262144

commit v7 on v6

--- a/solution.py
+++ b/solution.py
@@ -68,7 +68,7 @@
     sub_size, crs_size,
     mult_h, own_h, nbr_h, face_h, nlist_h, factor_h, out_h,
     mult, own, nbr, face, nlist, factor,
-    modes, pair, s_send, s_recv, slab, high, low, a_send, a_recv,
+    modes, pair, s_send, s_recv, slab, wide_f, a_send, a_recv,
     in_sem, f_ssem, f_rsem, s_ssem, s_rsem, a_ssem, a_rsem,
 ):
     nk, subs, width = own.shape
@@ -311,7 +311,7 @@
 
             def take(block, start, size):
                 at = block // 2 * LANES + block % 2 * held + start
-                return jnp.concatenate([high[at:at + size, :], low[at:at + size, :]], axis=1)
+                return jnp.concatenate(parted(slab[at:at + size, :]), axis=1)
 
             others = [take(n, p * part, part), take(q, p * part, part)]
             halves_of = [take(b, 0, held), jnp.concatenate(others if p == 0 else others[::-1], axis=0)]
@@ -333,7 +333,7 @@
         def _():
             landed(slab.at[pl.ds(0, sub_size * held), :], f_rsem)
 
-        high[...], low[...] = parted(slab[...])
+        wide_f[...] = both(slab[...], axis=1)
         landed(s_recv.at[pl.ds(0, devices - 1)], s_rsem)
         for b in range(sub_size):
             x, n, q = around(b)
@@ -347,8 +347,7 @@
                 rhs[q // 2] = rhs[q // 2] + only(turned(value, at - off), that + at, part)
                 rhs[x // 2] = rhs[x // 2] + only(turned(value, this + at - far), this + at, part)
         rhs_rows = jnp.concatenate(parted(jnp.concatenate(rhs, axis=1)), axis=0)
-        split = jnp.concatenate([high[...], low[...]], axis=1)
-        panel = quarters(dot(rhs_rows, split, NN))
+        panel = quarters(dot(rhs_rows.astype(jnp.bfloat16), wide_f[...], NN))
         ph, pw = parted(panel)
         wide = jnp.concatenate(
             [jnp.concatenate([ph, ph], axis=1), jnp.concatenate([pw, pw], axis=1)], axis=0)
@@ -357,7 +356,7 @@
         for d in range(crs_size):
             a_send[d] = term[:, d * LANES:(d + 1) * LANES]
             a_copy(jnp.int32(d)).start()
-        amps = halves(dot(wide, split, NT))
+        amps = halves(dot(wide.astype(jnp.bfloat16), wide_f[...], NT))
         tiled = [amps[:, i * LANES:(i + 1) * LANES] for i in range(sub_size // 2)]
 
         def form(d):
@@ -432,8 +431,7 @@
             pltpu.VMEM((nrhs, LANES), f32),
             pltpu.VMEM((devices, nrhs, LANES), f32),
             pltpu.VMEM((order, LANES), f32),
-            pltpu.VMEM((order, LANES), f32),
-            pltpu.VMEM((order, LANES), f32),
+            pltpu.VMEM((order, 2 * LANES), bf16),
             pltpu.VMEM((devices, nrhs, LANES), f32),
             pltpu.VMEM((slabs, nrhs, LANES), f32),
             dma((4,)), dma, dma, dma, dma, dma, dma,

time: 14.8 us -> 14.7 us (level)
  no operation moved by 1% of the time
where the time goes in v7:
time: 14.7 us; the launch traced here: 14.6 us
  Pallas kernels  13.9 us (95%)
  local copies, waits for them, and re-layouts  0.66 us (4%)
    pallas_call x1, Pallas kernels, near_body(): pl.pallas_call(functools.partial(near_kernel, sub_size, crs_size), out_sh...  13.9 us
    unnamed x1, local copies, waits for them, and re-layouts  0.66 us

profile of v7, /device:TPU:0, one launch (start us, length us, event | category | flops | bytes accessed | tf_op | source)
XLA Modules:
  0.0 14.6 jit_solution(13070934579727019658)
XLA Ops:
  0.0 13.9 %shard_map.64 = f32[16,4,512]{2,1,0:T(4,128)S(1)} custom-call(f32[16,4,512]{2,1,0:T(4,128)} %mult_h.1, f32[6,4,512]{2,1,0:T(4,128)} %own_h.1, f32[6,4,512]{2,1,0:T(4,128)} %nbr_h.1, s32[4,512]{1,0:T(4,128)} %face_h.1, s32[6,128]{1,0:T(8,128)} %bitcast.1, f32[48,384]{1,0:T(8,128)} %factor_h.1), custom_call_target="tpu_custom_call" | custom-call | tf_op jit(solution)/shard_map/pallas_call | solution.py:420
  13.9 0.7 %copy.8 = f32[16,4,512]{2,1,0:T(4,128)} copy(f32[16,4,512]{2,1,0:T(4,128)S(1)} %shard_map.64) | data formatting | bytes 262144
